TPU v7x, 32 devices: a whole 2x2x4 slice. The times are simulated.
32 devices in a mesh: batch: 4 (over y, x), field: 2 (over core), dim: 4 (over z).
Axes of the slice: x: 2, y: 2, z: 4, core: 2. Of those that a mesh axis runs over, the one named last changes fastest.
Arguments:
- features: bfloat16 [26, 128, 4096], P('field', 'dim', 'batch'), may hold values from -6 to 6
- cross_weight: bfloat16 [2, 26, 128, 26, 128], P(None, 'field', 'dim'), may hold values from -0.109375 to 0.109375
- cross_bias: float32 [2, 26, 128], P(None, 'field', 'dim'), may hold values from -3 to 3
- tower_weight: bfloat16 [1024, 26, 128], P(('field', 'dim')), may hold values from -0.109375 to 0.109375
- tower_bias: float32 [1024], P(('field', 'dim')), may hold values from -3 to 3
- query_weight: bfloat16 [1024, 128], P(('field', 'dim')), may hold values from -0.1875 to 0.1875
- user_vec: bfloat16 [4096, 128], P('batch'), may hold values from -6 to 6
- candidates: bfloat16 [1024, 128], P('batch'), may hold values from -6 to 6
- positive: int32 [4096], P('batch'), may hold values from 0 to 1023
Outputs:
- crossed: bfloat16 [26, 128, 4096], P('field', 'dim', 'batch')
- losses: float32 [4096], P('batch')
All inputs are finite; a program needn't handle non-finite values.
Results may differ from a plain program's by a relative error of at most 0.0049.
Values may be sent and summed in bfloat16 or wider, within the bound.
A program may use at most 64 MiB of HBM per device.

v0:
```python
import math

import jax
import jax.numpy as jnp
from jax import lax
from jax.sharding import PartitionSpec as P

CROSS = 2


def by_device(weights, field_count, dim_count):
    out_count, fields_all, entries_all = weights.shape
    shaped = weights.reshape(
        out_count, field_count, fields_all // field_count, dim_count, entries_all // dim_count
    )
    shaped = shaped.transpose(1, 3, 0, 2, 4)
    return shaped.reshape(
        field_count * dim_count, out_count, fields_all // field_count * (entries_all // dim_count)
    )


def row_adder(blocks, shards):
    return jnp.einsum("kib,koi->ob", shards, blocks, preferred_element_type=jnp.float32)


def cross_flat(current, blocks):
    field_local, entry_local, row_count = current.shape
    flattened = current.reshape(1, field_local * entry_local, row_count)
    return row_adder(blocks, lax.all_gather(flattened, ("field", "dim"), axis=0, tiled=True))


def next_layer(anchor, current, product, bias_vec):
    field_local, entry_local, row_count = current.shape
    gated = (product + bias_vec.reshape(field_local * entry_local, 1)).reshape(
        field_local, entry_local, row_count
    )
    return (anchor * gated + current.astype(jnp.float32)).astype(jnp.bfloat16)


def candidate_loss(query_vec, targets, candidates):
    score_scale = 1.0 / math.sqrt(query_vec.shape[1])
    row_count = query_vec.shape[0]
    running_max = jnp.full((row_count,), -1e30, jnp.float32)
    logits = (
        jnp.einsum(
            "be,ce->bc",
            query_vec,
            lax.all_gather(candidates, "batch", axis=0, tiled=True),
            preferred_element_type=jnp.float32,
        )
        * score_scale
    )
    labels = lax.broadcasted_iota(jnp.int32, logits.shape, 1)
    picked = jnp.sum(jnp.where(labels == targets[:, None], logits, 0.0), axis=1)
    new_max = jnp.maximum(running_max, jnp.max(logits, axis=1))
    running_sum = jnp.sum(jnp.exp(logits - new_max[:, None]), axis=1)
    best_score, exp_total, picked = (new_max, running_sum, picked)
    return best_score + jnp.log(exp_total) - picked


def body(
    features,
    cross_weight,
    cross_bias,
    tower_weight,
    tower_bias,
    query_weight,
    user_vec,
    candidates,
    positive,
):
    field_count = lax.axis_size("field")
    dim_count = lax.axis_size("dim")
    field_local, entry_local, row_count = features.shape
    column_count = field_local * entry_local
    anchor = features.astype(jnp.float32)
    current = features
    stacked = cross_weight.reshape(
        CROSS, column_count, cross_weight.shape[3], cross_weight.shape[4]
    )
    for level_idx in range(CROSS):
        blocks = by_device(stacked[level_idx], field_count, dim_count)
        product = cross_flat(current, blocks)
        current = next_layer(anchor, current, product, cross_bias[level_idx])
    tower_blocks = by_device(tower_weight, field_count, dim_count)
    flattened = current.reshape(1, column_count, row_count)
    tower_pre = row_adder(
        tower_blocks, lax.all_gather(flattened, ("field", "dim"), axis=0, tiled=True)
    )
    hidden = jax.nn.relu(tower_pre + tower_bias[:, None]).astype(jnp.bfloat16)
    partial_value = lax.dot_general(
        hidden, query_weight, (((0,), (0,)), ((), ())), preferred_element_type=jnp.float32
    )
    share_rows = row_count // (field_count * dim_count)
    member = lax.axis_index(("field", "dim"))
    query_part = lax.psum_scatter(
        partial_value.astype(jnp.bfloat16), ("field", "dim"), scatter_dimension=0, tiled=True
    ).astype(jnp.float32)
    user_rows = lax.dynamic_slice_in_dim(user_vec, member * share_rows, share_rows, 0)
    targets = lax.dynamic_slice_in_dim(positive, member * share_rows, share_rows, 0)
    query_vec = (query_part + user_rows.astype(jnp.float32)).astype(jnp.bfloat16)
    part_loss = candidate_loss(query_vec, targets, candidates)
    losses = lax.all_gather(part_loss, ("field", "dim"), axis=0, tiled=True)
    return (current, losses)


def solution(mesh):
    placed = (
        P("field", "dim", "batch"),
        P(None, "field", "dim", None, None),
        P(None, "field", "dim"),
        P(("field", "dim"), None, None),
        P(("field", "dim")),
        P(("field", "dim"), None),
        P("batch", None),
        P("batch", None),
        P("batch"),
    )
    return jax.shard_map(
        body,
        mesh=mesh,
        in_specs=placed,
        out_specs=(P("field", "dim", "batch"), P("batch")),
        check_vma=False,
    )
```

profile of v0, /device:TPU:0, one launch (start us, length us, event | category | flops | bytes accessed | tf_op | source)
XLA Modules:
  0.0 289.6 jit_solution(7314092059662878621)
XLA Ops:
  7.2 0.0 copy-start
  7.2 0.0 all-gather.5.cloned.1.call-start
  7.2 0.7 all-gather.5.cloned.1.call-update
  7.9 0.0 all-gather.7.cloned.1.call-start
  8.0 3.6 %fusion.13 = (bf16[1,13,32,26,128]{4,2,3,1,0:T(8,128)(2,1)S(1)}, bf16[1,13,32,26,128]{4,2,3,1,0:T(8,128)(2,1)S(1)}) fusion(bf16[2,13,32,26,128]{4,2,3,1,0:T(8,128)(2,1)} %param.10), kind=kLoop, calls=%fused_computation.27 | loop fusion | bytes 11075584 | tf_op jit(solution)/shard_map/slice | solution.py:82
  11.5 2.0 copy.19
  13.5 15.0 %reshape_squeeze.8 = bf16[416,2,13,4,32]{4,3,0,2,1:T(4,128)(2,1)} reshape(bf16[1,13,32,26,128]{4,2,1,3,0:T(8,128)(2,1)} %copy.19) | data formatting | bytes 5537792 | tf_op jit(solution)/shard_map/reshape;squeeze | solution.py:13
  28.6 0.0 copy-start.6
  28.6 18.5 %copy.20 = bf16[2,4,416,13,32]{2,4,3,1,0:T(8,128)(2,1)} copy(bf16[2,4,416,13,32]{4,1,2,3,0:T(4,128)(2,1)} %bitcast.50) | data formatting | bytes 5537792 | tf_op jit(solution)/shard_map/transpose | solution.py:16
  47.1 0.0 copy-done.6
  47.1 0.1 add.53
  47.2 34.2 %all-gather.5.cloned.1.call-done = bf16[8,416,1024]{2,1,0:T(8,128)(2,1)} async-done(((bf16[1,416,1024]{2,1,0:T(8,128)(2,1)}), bf16[8,416,1024]{2,1,0:T(8,128)(2,1)}) %all-gather.5.cloned.1.call-update) | async-done | bytes 6815760 | tf_op jit(solution)/shard_map/all_gather | solution.py:29
  81.4 0.0 copy-start.1
  81.4 6.4 %bitcast_add_fusion.1 = f32[416,1024]{1,0:T(8,128)S(1)} fusion(bf16[8,416,416]{1,2,0:T(8,128)(2,1)} %bitcast.54, bf16[8,416,1024]{2,1,0:T(8,128)(2,1)} %all-gather.5.cloned.1.call-done, f32[416]{0:T(512)S(1)} %add.53), kind=kOutput, calls=%fused_computation.6 | convolution fusion | flops 2835775488 | bytes 11290240 | tf_op jit(solution)/shard_map/kib,koi->ob/dot_general | solution.py:23
  87.7 0.0 copy-done.1
  87.8 1.2 fusion.2
  88.9 0.0 all-gather.7.cloned.1.call-update
  89.0 0.0 all-gather.9.cloned.1.call-start
  89.0 2.0 copy.22
  91.0 15.0 %reshape_squeeze.9 = bf16[416,2,13,4,32]{4,3,0,2,1:T(4,128)(2,1)} reshape(bf16[1,13,32,26,128]{4,2,1,3,0:T(8,128)(2,1)} %copy.22) | data formatting | bytes 5537792 | tf_op jit(solution)/shard_map/reshape;squeeze | solution.py:13
  106.0 16.8 %copy.23 = bf16[2,4,416,13,32]{2,4,3,1,0:T(8,128)(2,1)S(1)} copy(bf16[2,4,416,13,32]{4,1,2,3,0:T(4,128)(2,1)} %bitcast.51) | data formatting | bytes 5537792 | tf_op jit(solution)/shard_map/transpose | solution.py:16
  122.8 0.1 add.57
  122.9 33.8 %all-gather.7.cloned.1.call-done = bf16[8,416,1024]{2,1,0:T(8,128)(2,1)} async-done(((bf16[1,416,1024]{2,1,0:T(8,128)(2,1)}), bf16[8,416,1024]{2,1,0:T(8,128)(2,1)}) %all-gather.7.cloned.1.call-update) | async-done | bytes 6815760 | tf_op jit(solution)/shard_map/all_gather | solution.py:29
  156.8 0.0 copy-start.2
  156.8 0.0 copy-start.3
  156.8 5.4 %bitcast_add_fusion = f32[1024,416]{0,1:T(8,128)S(1)} fusion(bf16[8,416,1024]{2,1,0:T(8,128)(2,1)} %all-gather.7.cloned.1.call-done, bf16[8,416,416]{1,2,0:T(8,128)(2,1)S(1)} %bitcast.55, f32[416]{0:T(512)S(1)} %add.57), kind=kOutput, calls=%fused_computation.5 | convolution fusion | flops 2835775488 | bytes 11290240 | tf_op jit(solution)/shard_map/kib,koi->ob/dot_general | solution.py:23
  162.2 0.0 copy-start.4
  162.2 0.0 copy-done.2
  162.2 0.0 copy-done.3
  162.2 0.0 copy-start.7
  162.2 1.3 fusion.1
  163.6 0.0 all-gather.9.cloned.1.call-update
  163.6 0.0 reduce-scatter.2.cloned.1.call-start
  163.6 0.0 copy-done.4
  163.6 0.6 copy.25
  164.3 0.1 copy.26
  164.3 67.0 %all-gather.9.cloned.1.call-done = bf16[8,416,1024]{2,1,0:T(8,128)(2,1)} async-done(((bf16[1,416,1024]{2,1,0:T(8,128)(2,1)}), bf16[8,416,1024]{2,1,0:T(8,128)(2,1)}) %all-gather.9.cloned.1.call-update) | async-done | bytes 6815760 | tf_op jit(solution)/shard_map/all_gather | solution.py:88
  231.4 0.0 copy-done
  231.4 0.0 copy-done.7
  231.4 0.0 copy-start.5
  231.4 5.8 %fusion.7 = bf16[1024,128]{1,0:T(8,128)(2,1)} fusion(bf16[128,128]{1,0:T(8,128)(2,1)S(1)} %copy-done, bf16[8,416,1024]{2,1,0:T(8,128)(2,1)} %all-gather.9.cloned.1.call-done, bf16[8,128,416]{1,2,0:T(8,128)(2,1)S(1)} %bitcast.60, f32[128]{0:T(128)S(1)} %copy-done.7), kind=kOutput, calls=%fused_computation.13 | convolution fusion | flops 906493952 | bytes 7963136 | tf_op jit(solution)/shard_map/dot_general | solution.py:91
  237.2 0.0 reduce-scatter.2.cloned.1.call-update
  237.2 0.8 dynamic_slice.7
  238.0 0.0 copy-done.5
  238.0 8.9 %all_gather.18 = bf16[1024,128]{1,0:T(8,128)(2,1)S(1)} all-gather(bf16[256,128]{1,0:T(8,128)(2,1)S(1)} %copy-done.5), channel_id=1, replica_groups=mesh['batch'=4,'field'=2,'dim'=4] {'batch'}, dimensions={0}, use_global_device_ids=true | all-gather | bytes 327680 | tf_op jit(solution)/shard_map/all_gather | solution.py:48
  246.9 20.9 %reduce-scatter.2.cloned.1.call-done = bf16[128,128]{1,0:T(8,128)(2,1)} async-done(((bf16[1024,128]{1,0:T(8,128)(2,1)}), bf16[128,128]{1,0:T(8,128)(2,1)}) %reduce-scatter.2.cloned.1.call-update) | async-done | bytes 32784 | tf_op jit(solution)/shard_map/reduce_scatter | solution.py:96
  267.9 1.1 fusion.14
  269.0 0.3 exponential_reduce_fusion
  269.2 13.2 %all-gather = f32[8,1,128]{2,1,0:T(1,128)S(1)} all-gather(f32[1,1,128]{2,1,0:T(1,128)S(1)} %subtract_bitcast_fusion), channel_id=1, replica_groups=mesh['batch'=4,'field'=2,'dim'=4] {'field','dim'}, dimensions={0}, use_global_device_ids=true | all-gather | bytes 4608 | tf_op jit(solution)/shard_map/all_gather | solution.py:103
  282.5 0.6 copy.30
  (3 shorter events, 0.1 us)
Async XLA Ops:
  7.2 224.2 %copy-start = (bf16[128,128]{1,0:T(8,128)(2,1)S(1)}, bf16[128,128]{1,0:T(8,128)(2,1)}, u32[]{:S(2)}) copy-start(bf16[128,128]{1,0:T(8,128)(2,1)} %param.14) | copy-start | bytes 98308
  7.2 74.2 %all-gather.5.cloned.1.call-start = ((), (), s32[]{:S(2)}) async-start(), calls=%async_computation.1 | async-start | bytes 7667712 | tf_op jit(solution)/shard_map/all_gather | solution.py:29
  7.9 148.8 %all-gather.7.cloned.1.call-start = ((), (), s32[]{:S(2)}) async-start(), calls=%async_computation.2 | async-start | bytes 7667712 | tf_op jit(solution)/shard_map/all_gather | solution.py:29
  28.6 18.5 %copy-start.6 = (f32[2,13,32]{2,0,1:T(2,128)S(1)}, f32[2,13,32]{2,0,1:T(2,128)}, u32[]{:S(2)}) copy-start(f32[2,13,32]{2,0,1:T(2,128)} %param.11) | copy-start | bytes 9988
  81.4 6.4 %copy-start.1 = (bf16[13,32,1024]{2,1,0:T(8,128)(2,1)S(1)}, bf16[13,32,1024]{2,1,0:T(8,128)(2,1)}, u32[]{:S(2)}) copy-start(bf16[13,32,1024]{2,1,0:T(8,128)(2,1)} %param.9) | copy-start | bytes 2555908
  89.0 142.4 %all-gather.9.cloned.1.call-start = ((), (), s32[]{:S(2)}) async-start(), calls=%async_computation.3 | async-start | bytes 7667712 | tf_op jit(solution)/shard_map/all_gather | solution.py:88
  156.8 5.4 %copy-start.2 = (bf16[13,32,1024]{2,1,0:T(8,128)(2,1)S(1)}, bf16[13,32,1024]{2,1,0:T(8,128)(2,1)}, u32[]{:S(2)}) copy-start(bf16[13,32,1024]{2,1,0:T(8,128)(2,1)} %param.9) | copy-start | bytes 2555908
  156.8 5.4 %copy-start.3 = (bf16[13,32,1024]{2,1,0:T(8,128)(2,1)S(1)}, bf16[13,32,1024]{2,1,0:T(8,128)(2,1)}, u32[]{:S(2)}) copy-start(bf16[13,32,1024]{2,1,0:T(8,128)(2,1)} %fusion.2) | copy-start | bytes 2555908
  162.2 1.5 copy-start.4
  162.2 69.2 %copy-start.7 = (f32[128]{0:T(128)S(1)}, f32[128]{0:T(128)}, u32[]{:S(2)}) copy-start(f32[128]{0:T(128)} %param.13) | copy-start | bytes 1540
  163.6 104.3 %reduce-scatter.2.cloned.1.call-start = ((), (), s32[]{:S(2)}) async-start(), calls=%async_computation.4 | async-start | bytes 294912 | tf_op jit(solution)/shard_map/reduce_scatter | solution.py:96
  231.4 6.6 %copy-start.5 = (bf16[256,128]{1,0:T(8,128)(2,1)S(1)}, bf16[256,128]{1,0:T(8,128)(2,1)}, u32[]{:S(2)}) copy-start(bf16[256,128]{1,0:T(8,128)(2,1)} %param.16) | copy-start | bytes 196612
Sparse Core Ops, SparseCore 0:
  9.6 71.7 all-gather.4
  89.1 67.6 all-gather.6
  163.7 67.6 all-gather.8
  237.4 30.4 reduce-scatter.1
where the time goes:
time: 291 us; the launch traced here: 290 us
  waiting for transfers between devices  157 us (54%)
  local copies, waits for them, and re-layouts  75.2 us (26%)
  blocking collectives  22.2 us (8%)
  matrix products  18.7 us (6%)
  between operations  13.9 us (5%)
    all_gather x2, waiting for transfers between devices, cross_flat(): lax.all_gather(flattened, ('field', 'dim'), axis=0, tiled=True)  68 us
    all_gather x1, waiting for transfers between devices, body(): lax.all_gather(flattened, ('field', 'dim'), axis=0, tiled=True)  67 us
    transpose x3, local copies, waits for them, and re-layouts, by_device(): shaped = shaped.transpose(1, 3, 0, 2, 4)  35.3 us
    another operation x2, local copies, waits for them, and re-layouts, by_device(): weights.reshape(out_count, field_count, fields_all // field_count, dim_co...  30.1 us
    reduce_scatter x1, waiting for transfers between devices, body(): lax.psum_scatter(partial_value.astype(jnp.bfloat16), ('field', 'dim'), sc...  20.9 us
    all_gather x1, blocking collectives, body(): losses = lax.all_gather(part_loss, ('field', 'dim'), axis=0, tiled=True)  13.2 us
    dot_general x2, matrix products, row_adder(): jnp.einsum('kib,koi->ob', shards, blocks, preferred_element_type=jnp.floa...  11.8 us
    all_gather x1, blocking collectives, candidate_loss(): lax.all_gather(candidates, 'batch', axis=0, tiled=True)  8.93 us
  transfers between devices with their start and end apart: 4, of which 4 were waited for; matrix products, arithmetic and copies ran while one was open for 26% of the time, Pallas kernels for 0%

commit v1 on v0

v1 whole, which is shorter than its diff:
```python
import functools
import math

import jax
import jax.numpy as jnp
from jax import lax
from jax.experimental import pallas as pl
from jax.experimental.pallas import tpu as pltpu
from jax.sharding import PartitionSpec as P

CROSS = 2
MESH = pl.DeviceIdType.MESH


def chunk_count(row_count, member_count):
    chunks = 4
    while chunks > 1 and (row_count % (chunks * 128) or member_count % chunks):
        chunks //= 2
    return chunks


def cross_kernel(
    field_count, dim_count, chunks, feat, weight, bias, out, rows_out,
    x0, x1, raw, flat, stage, sent, rows,
    feat_sem, weight_sem, right_sem, left_sem, pair_sem, recv_sem, pair_recv, row_send, row_recv,
):
    f = lax.axis_index("field")
    d = lax.axis_index("dim")
    me = f * dim_count + d
    members = field_count * dim_count
    fl, el, row_count = feat.shape
    columns = fl * el
    fields, width, rc = x0.shape[1:]
    share = row_count // members
    per_chunk = members // chunks
    buffers = (x0, x1)
    other = field_count - 1 - f
    to_right = jnp.minimum(d + 1, dim_count - 1)
    to_left = jnp.maximum(d - 1, 0)

    def place(ff, o):
        return pl.ds(ff * fl, fl), pl.ds(pl.multiple_of(o * el, el), el)

    def piece(buffer, c, ff, o):
        fs, ds = place(ff, o)
        return buffer.at[c, fs, ds, :]

    def right(ph, c, o):
        ref = piece(buffers[ph], c, f, o)
        return pltpu.make_async_remote_copy(
            ref, ref, right_sem.at[ph, c, o], recv_sem.at[ph, c, o],
            device_id={"dim": to_right}, device_id_type=MESH)

    def left(ph, c, o):
        ref = piece(buffers[ph], c, f, o)
        return pltpu.make_async_remote_copy(
            ref, ref, left_sem.at[ph, c, o], recv_sem.at[ph, c, o],
            device_id={"dim": to_left}, device_id_type=MESH)

    def pair(ph, c, o, ff):
        ref = piece(buffers[ph], c, ff, o)
        return pltpu.make_async_remote_copy(
            ref, ref, pair_sem.at[ph, c, o], pair_recv.at[ph, c, o],
            device_id={"field": other}, device_id_type=MESH)

    def issue_own(ph, c):
        @pl.when(d < dim_count - 1)
        def _():
            right(ph, c, d).start()

        @pl.when(d > 0)
        def _():
            left(ph, c, d).start()

        pair(ph, c, d, f).start()

    def forwards(ph, c):
        for s in range(1, dim_count):
            @pl.when(d - s >= 0)
            def _():
                right(ph, c, d - s).wait_recv()

                @pl.when(d < dim_count - 1)
                def _():
                    right(ph, c, d - s).start()

                pair(ph, c, d - s, f).start()

            @pl.when(d + s < dim_count)
            def _():
                left(ph, c, d + s).wait_recv()

                @pl.when(d > 0)
                def _():
                    left(ph, c, d + s).start()

                pair(ph, c, d + s, f).start()
        for o in range(dim_count):
            pair(ph, c, o, other).wait_recv()

    def relayout(level):
        pltpu.make_async_copy(weight.at[level], raw.at[level], weight_sem.at[level]).wait()

        def group(g, carry):
            base = pl.multiple_of(g * 16, 16)
            for i in range(16):
                stage[i * 32:i * 32 + fields, :] = raw[level, base + i].astype(jnp.float32)
            for ff in range(fields):
                flat[level, pl.ds(base, 16), ff * width:(ff + 1) * width] = stage[
                    pl.ds(ff, 16, stride=32), :].astype(jnp.bfloat16)
            return carry

        lax.fori_loop(0, columns // 16, group, 0)

    def advance(ph, c):
        whole = buffers[ph][c].reshape(fields * width, rc)
        product = jnp.dot(flat[ph], whole, preferred_element_type=jnp.float32) + bias[ph]
        fs, ds = place(f, d)
        anchor = x0[c, fs, ds, :].astype(jnp.float32).reshape(columns, rc)
        current = buffers[ph][c, fs, ds, :].astype(jnp.float32).reshape(columns, rc)
        return (anchor * product + current).astype(jnp.bfloat16).reshape(fl, el, rc)

    def row_copy(m):
        fs, ds = place(f, d)
        return pltpu.make_async_remote_copy(
            sent.at[m], rows.at[fs, ds, :], row_send.at[m], row_recv.at[me],
            device_id={"field": m // dim_count, "dim": m % dim_count}, device_id_type=MESH)

    own_copies = []
    for c in range(chunks):
        copy = pltpu.make_async_copy(
            feat.at[:, :, pl.ds(c * rc, rc)], piece(x0, c, f, d), feat_sem.at[c])
        copy.start()
        own_copies.append(copy)
    for level in range(CROSS):
        pltpu.make_async_copy(weight.at[level], raw.at[level], weight_sem.at[level]).start()

    barrier = pltpu.get_barrier_semaphore()
    for k in range(1, members):
        m = lax.rem(me + k, members)
        pl.semaphore_signal(
            barrier, inc=1, device_id={"field": m // dim_count, "dim": m % dim_count},
            device_id_type=MESH)
    pl.semaphore_wait(barrier, members - 1)
    for copy in own_copies:
        copy.wait()
    issue_own(0, 0)
    if chunks > 1:
        issue_own(0, 1)
    relayout(0)

    def first(c, carry):
        forwards(0, c)
        fs, ds = place(f, d)
        x1[c, fs, ds, :] = advance(0, c)
        issue_own(1, c)

        @pl.when(c + 2 < chunks)
        def _():
            issue_own(0, c + 2)

        return carry

    lax.fori_loop(0, chunks, first, 0)
    relayout(1)

    def second(c, carry):
        forwards(1, c)
        new = advance(1, c)
        out[:, :, pl.ds(pl.multiple_of(c * rc, 128), rc)] = new
        for j in range(per_chunk):
            m = c * per_chunk + j
            part = new[:, :, j * share:(j + 1) * share]

            @pl.when(m == me)
            def _():
                fs, ds = place(f, d)
                rows[fs, ds, :] = part

            @pl.when(m != me)
            def _():
                sent[m] = part
                row_copy(m).start()

        return carry

    lax.fori_loop(0, chunks, second, 0)

    for k in range(1, members):
        m = lax.rem(me + k, members)
        fs, ds = place(m // dim_count, m % dim_count)
        ref = rows.at[fs, ds, :]
        pltpu.make_async_remote_copy(
            sent.at[m], ref, row_send.at[m], row_recv.at[m],
            device_id={"field": m // dim_count, "dim": m % dim_count}, device_id_type=MESH,
        ).wait_recv()
        row_copy(m).wait_send()
    rows_out[...] = rows[...]

    def drain(c, carry):
        for ph in range(CROSS):
            for o in range(dim_count):
                @pl.when((o <= d) & (d < dim_count - 1))
                def _():
                    right(ph, c, o).wait_send()

                @pl.when((o >= d) & (d > 0))
                def _():
                    left(ph, c, o).wait_send()

                pair(ph, c, o, f).wait_send()
        return carry

    lax.fori_loop(0, chunks, drain, 0)


def cross_layers(features, cross_weight, cross_bias):
    field_count = lax.axis_size("field")
    dim_count = lax.axis_size("dim")
    members = field_count * dim_count
    fl, el, row_count = features.shape
    columns = fl * el
    fields, width = cross_weight.shape[3:]
    chunks = chunk_count(row_count, members)
    rc = row_count // chunks
    share = row_count // members
    steps = (CROSS, chunks, dim_count)
    dma = pltpu.SemaphoreType.DMA
    return pl.pallas_call(
        functools.partial(cross_kernel, field_count, dim_count, chunks),
        out_shape=(
            jax.ShapeDtypeStruct(features.shape, jnp.bfloat16),
            jax.ShapeDtypeStruct((fields, width, share), jnp.bfloat16),
        ),
        in_specs=[
            pl.BlockSpec(memory_space=pl.ANY),
            pl.BlockSpec(memory_space=pl.ANY),
            pl.BlockSpec(memory_space=pltpu.VMEM),
        ],
        out_specs=(
            pl.BlockSpec(memory_space=pltpu.VMEM),
            pl.BlockSpec(memory_space=pltpu.VMEM),
        ),
        scratch_shapes=[
            pltpu.VMEM((chunks, fields, width, rc), jnp.bfloat16),
            pltpu.VMEM((chunks, fields, width, rc), jnp.bfloat16),
            pltpu.VMEM((CROSS, columns, fields, width), jnp.bfloat16),
            pltpu.VMEM((CROSS, columns, fields * width), jnp.bfloat16),
            pltpu.VMEM((16 * 32, width), jnp.float32),
            pltpu.VMEM((members, fl, el, share), jnp.bfloat16),
            pltpu.VMEM((fields, width, share), jnp.bfloat16),
            dma((chunks,)),
            dma((CROSS,)),
            dma(steps),
            dma(steps),
            dma(steps),
            dma(steps),
            dma(steps),
            dma((members,)),
            dma((members,)),
        ],
        compiler_params=pltpu.CompilerParams(
            collective_id=0, has_side_effects=True, vmem_limit_bytes=52 * 2**20),
        cost_estimate=pl.CostEstimate(
            flops=4 * columns * fields * width * row_count,
            bytes_accessed=400_000_000, transcendentals=0),
        name="cross_layers",
    )(
        features,
        cross_weight.reshape(CROSS, columns, fields, width),
        cross_bias.reshape(CROSS, columns, 1),
    )


def spread(block):
    units = block.shape[0]
    batch_count = lax.axis_size("batch")
    split = batch_count if units % (batch_count * 16) == 0 else 1
    if split == 1:
        return lax.all_gather(block, ("field", "dim"), axis=0, tiled=True), split
    part = units // split
    mine = lax.dynamic_slice_in_dim(block, lax.axis_index("batch") * part, part, 0)
    level = lax.all_gather(mine, ("field", "dim"), axis=0, tiled=True)
    return lax.all_gather(level, "batch", axis=0, tiled=True), split


def regroup(whole, members, split):
    shaped = whole.reshape((members, split, -1) + whole.shape[1:])
    return jnp.swapaxes(shaped, 0, 1).reshape(whole.shape)


def body(
    features, cross_weight, cross_bias, tower_weight, tower_bias, query_weight,
    user_vec, candidates, positive,
):
    members = lax.axis_size("field") * lax.axis_size("dim")
    row_count = features.shape[2]
    fields, width = tower_weight.shape[1:]
    tower_all, split = spread(tower_weight.reshape(-1, fields * width))
    query_all = lax.all_gather(query_weight, ("field", "dim"), axis=0, tiled=True)
    bias_all = lax.all_gather(tower_bias, ("field", "dim"), axis=0, tiled=True)
    query_all = regroup(query_all, members, split)
    bias_all = regroup(bias_all, members, split)
    candidates_all = lax.all_gather(candidates, "batch", axis=0, tiled=True)
    crossed, rows = cross_layers(features, cross_weight, cross_bias)
    share = row_count // members
    start = lax.axis_index(("field", "dim")) * share
    tower_pre = jnp.dot(
        tower_all, rows.reshape(fields * width, share), preferred_element_type=jnp.float32)
    hidden = jax.nn.relu(tower_pre + bias_all[:, None]).astype(jnp.bfloat16)
    query = lax.dot_general(
        hidden, query_all, (((0,), (0,)), ((), ())), preferred_element_type=jnp.float32)
    user_rows = lax.dynamic_slice_in_dim(user_vec, start, share, 0)
    targets = lax.dynamic_slice_in_dim(positive, start, share, 0)
    query_vec = (query + user_rows.astype(jnp.float32)).astype(jnp.bfloat16)
    logits = lax.dot_general(
        query_vec, candidates_all, (((1,), (1,)), ((), ())), preferred_element_type=jnp.float32
    ) * (1.0 / math.sqrt(query_vec.shape[1]))
    labels = lax.broadcasted_iota(jnp.int32, logits.shape, 1)
    picked = jnp.sum(jnp.where(labels == targets[:, None], logits, 0.0), axis=1)
    best = jnp.max(logits, axis=1)
    total = jnp.sum(jnp.exp(logits - best[:, None]), axis=1)
    part_loss = best + jnp.log(total) - picked
    losses = lax.all_gather(part_loss, ("field", "dim"), axis=0, tiled=True)
    return (crossed, losses)


def solution(mesh):
    placed = (
        P("field", "dim", "batch"),
        P(None, "field", "dim", None, None),
        P(None, "field", "dim"),
        P(("field", "dim"), None, None),
        P(("field", "dim")),
        P(("field", "dim"), None),
        P("batch", None),
        P("batch", None),
        P("batch"),
    )
    return jax.shard_map(
        body,
        mesh=mesh,
        in_specs=placed,
        out_specs=(P("field", "dim", "batch"), P("batch")),
        check_vma=False,
    )
```

time: 291 us -> 278 us (0.955)
  Pallas kernels: 0 us -> 150 us
  waiting for transfers between devices: 157 us -> 28.9 us
  local copies, waits for them, and re-layouts: 75.2 us -> 14.4 us
  blocking collectives: 22.2 us -> 63.7 us
  matrix products: 18.7 us -> 6.33 us
    pallas_call x0 -> x1, Pallas kernels: none -> 150 us  [cross_layers(): pl.pallas_call(functools.partial(cross_kernel, field_count, dim_count, ch...]
    all_gather x3 -> x2, waiting for transfers between devices: 135 us -> 28.8 us  [the longest x1 28.8 us: spread(): level = lax.all_gather(mine, ('field', 'dim'), axis=0, tiled=True)]
    all_gather x1 -> x3, blocking collectives: 8.93 us -> 50.9 us  [the longest x1 25.1 us: body(): lax.all_gather(query_weight, ('field', 'dim'), axis=0, tiled=True)]
    transpose x3 -> x1, local copies, waits for them, and re-layouts: 35.3 us -> 0.02 us  [regroup(): return jnp.swapaxes(shaped, 0, 1).reshape(whole.shape)]
    another operation x2 -> x0, local copies, waits for them, and re-layouts: 30.1 us -> none  [by_device(): weights.reshape(out_count, field_count, fields_all // field_count, dim_co...]
    reduce_scatter x1 -> x0, waiting for transfers between devices: 20.9 us -> none  [body(): lax.psum_scatter(partial_value.astype(jnp.bfloat16), ('field', 'dim'), sc...]
    dot_general x4 -> x2, matrix products: 18.7 us -> 6.33 us  [the longest x1 5.04 us: body(): jnp.dot(tower_all, rows.reshape(fields * width, share), preferred_element...]
    unnamed x18 -> x13, local copies, waits for them, and re-layouts: 1.26 us -> 11.3 us
  transfers between devices with their start and end apart: 4 -> 2, of which waited for: 4 -> 1; matrix products, arithmetic and copies ran while one was open for 26% -> 4% of each run, Pallas kernels for 0% -> 54%
where the time goes in v1:
time: 278 us
  Pallas kernels  150 us (54%)
  blocking collectives  63.7 us (23%)
  waiting for transfers between devices  28.9 us (10%)
  local copies, waits for them, and re-layouts  14.4 us (5%)
  between operations  14.1 us (5%)
  matrix products  6.33 us (2%)
    pallas_call x1, Pallas kernels, cross_layers(): pl.pallas_call(functools.partial(cross_kernel, field_count, dim_count, ch...  150 us
    all_gather x1, waiting for transfers between devices, spread(): level = lax.all_gather(mine, ('field', 'dim'), axis=0, tiled=True)  28.8 us
    all_gather x1, blocking collectives, body(): lax.all_gather(query_weight, ('field', 'dim'), axis=0, tiled=True)  25.1 us
    all_gather x1, blocking collectives, body(): bias_all = lax.all_gather(tower_bias, ('field', 'dim'), axis=0, tiled=True)  16.5 us
    all_gather x1, blocking collectives, body(): losses = lax.all_gather(part_loss, ('field', 'dim'), axis=0, tiled=True)  12.8 us
    unnamed x13, local copies, waits for them, and re-layouts  11.3 us
    all_gather x1, blocking collectives, body(): candidates_all = lax.all_gather(candidates, 'batch', axis=0, tiled=True)  9.29 us
  transfers between devices with their start and end apart: 2, of which 1 were waited for; matrix products, arithmetic and copies ran while one was open for 4% of the time, Pallas kernels for 54%

profile of v1, /device:TPU:0, one launch (start us, length us, event | category | flops | bytes accessed | tf_op | source)
XLA Modules:
  0.0 278.2 jit_solution(8515029238619831720)
XLA Ops:
  7.2 0.0 all-gather.5.cloned.1.call-start
  7.2 1.6 copy.27
  8.8 0.3 constant_dynamic-slice_fusion
  9.1 1.0 copy.28
  10.1 0.0 all-gather.5.cloned.1.call-update
  10.1 0.0 all-gather.7.cloned.1.call-start
  10.1 28.8 %all-gather.5.cloned.1.call-done = bf16[256,3328]{1,0:T(8,128)(2,1)} async-done(((bf16[32,3328]{1,0:T(8,128)(2,1)}), bf16[256,3328]{1,0:T(8,128)(2,1)}) %all-gather.5.cloned.1.call-update) | async-done | bytes 1703952 | tf_op jit(solution)/shard_map/all_gather | solution.py:283
  39.0 0.0 copy-start.2
  39.0 0.0 all-gather.7.cloned.1.call-update
  39.0 8.2 %copy.24 = bf16[2,13,32,26,128]{4,3,2,1,0:T(8,128)(2,1)} copy(bf16[2,13,32,26,128]{4,2,3,1,0:T(8,128)(2,1)} %param.10) | data formatting | bytes 11075584 | tf_op args[1]
  47.2 0.0 copy-done.2
  47.2 0.4 reshape.40.bias
  47.6 0.0 copy-start.3
  47.6 0.0 copy-start.1
  47.6 0.0 copy-start
  47.7 149.7 %cross_layers.1 = (bf16[13,32,1024]{2,1,0:T(8,128)(2,1)S(1)}, bf16[26,128,128]{2,1,0:T(8,128)(2,1)}) custom-call(bf16[13,32,1024]{2,1,0:T(8,128)(2,1)} %feat.1, bf16[2,416,26,128]{3,2,1,0:T(8,128)(2,1)} %bitcast.19, f32[2,416,1]{2,1,0:T(8,128)S(1)} %reshape.40.bias), custom_call_target="tpu_custom_call" | custom-call | flops 5670699008 | bytes 400000000 | tf_op jit(solution)/shard_map/cross_layers/pallas_call | solution.py:229
  197.4 0.0 copy-done.3
  197.4 16.5 %all-gather = f32[8,1,128]{2,1,0:T(1,128)S(1)} all-gather(f32[1,1,128]{2,1,0:T(1,128)S(1)} %bitcast.25), channel_id=1, replica_groups=mesh['batch'=4,'field'=2,'dim'=4] {'field','dim'}, dimensions={0}, use_global_device_ids=true | all-gather | bytes 4608 | tf_op jit(solution)/shard_map/all_gather | solution.py:301
  213.9 0.5 broadcast.5
  214.4 0.7 reduce.3
  215.1 0.1 reshape.32
  215.1 0.1 add.27
  215.2 0.0 copy-done.1
  215.2 25.1 %all_gather.21 = bf16[1024,128]{1,0:T(8,128)(2,1)S(1)} all-gather(bf16[128,128]{1,0:T(8,128)(2,1)S(1)} %copy-done.1), channel_id=1, replica_groups=mesh['batch'=4,'field'=2,'dim'=4] {'field','dim'}, dimensions={0}, use_global_device_ids=true | all-gather | bytes 294912 | tf_op jit(solution)/shard_map/all_gather | solution.py:300
  240.4 0.8 dynamic_slice.11
  241.1 0.0 copy-done
  241.1 9.3 %all_gather.22 = bf16[1024,128]{1,0:T(8,128)(2,1)S(1)} all-gather(bf16[256,128]{1,0:T(8,128)(2,1)S(1)} %copy-done), channel_id=1, replica_groups=mesh['batch'=4,'field'=2,'dim'=4] {'batch'}, dimensions={0}, use_global_device_ids=true | all-gather | bytes 327680 | tf_op jit(solution)/shard_map/all_gather | solution.py:304
  250.4 0.0 all-gather.7.cloned.1.call-done
  250.4 5.0 %fusion.1 = bf16[1024,128]{1,0:T(8,128)(2,1)S(1)} fusion(bf16[1024,3328]{1,0:T(8,128)(2,1)} %all-gather.7.cloned.1.call-done, bf16[3328,128]{1,0:T(8,128)(2,1)} %bitcast.26, f32[1024]{0:T(1024)S(1)} %add.27), kind=kOutput, calls=%fused_computation.3 | convolution fusion | flops 872808448 | bytes 7933952 | tf_op jit(solution)/shard_map/dot_general | solution.py:308
  255.5 1.3 fusion.6
  256.8 0.3 exponential_reduce_fusion
  257.1 12.8 %all-gather.1 = f32[8,1,128]{2,1,0:T(1,128)S(1)} all-gather(f32[1,1,128]{2,1,0:T(1,128)S(1)} %subtract_bitcast_fusion), channel_id=1, replica_groups=mesh['batch'=4,'field'=2,'dim'=4] {'field','dim'}, dimensions={0}, use_global_device_ids=true | all-gather | bytes 4608 | tf_op jit(solution)/shard_map/all_gather | solution.py:324
  269.8 0.9 copy.35
  270.7 0.6 copy.36
  (4 shorter events, 0.0 us)
Async XLA Ops:
  7.2 31.8 %all-gather.5.cloned.1.call-start = ((), (), s32[]{:S(2)}) async-start(), calls=%async_computation | async-start | bytes 1916928 | tf_op jit(solution)/shard_map/all_gather | solution.py:283
  10.1 240.4 %all-gather.7.cloned.1.call-start = ((), (), s32[]{:S(2)}) async-start(), calls=%async_computation.1 | async-start | bytes 8519680 | tf_op jit(solution)/shard_map/all_gather | solution.py:284
  39.0 8.2 %copy-start.2 = (f32[2,13,32]{2,0,1:T(2,128)S(1)}, f32[2,13,32]{2,0,1:T(2,128)}, u32[]{:S(2)}) copy-start(f32[2,13,32]{2,0,1:T(2,128)} %param.11) | copy-start | bytes 9988
  47.6 149.8 %copy-start.3 = (f32[128]{0:T(128)S(1)}, f32[128]{0:T(128)}, u32[]{:S(2)}) copy-start(f32[128]{0:T(128)} %param.13) | copy-start | bytes 1540
  47.6 167.6 %copy-start.1 = (bf16[128,128]{1,0:T(8,128)(2,1)S(1)}, bf16[128,128]{1,0:T(8,128)(2,1)}, u32[]{:S(2)}) copy-start(bf16[128,128]{1,0:T(8,128)(2,1)} %param.14) | copy-start | bytes 98308
  47.6 193.5 %copy-start = (bf16[256,128]{1,0:T(8,128)(2,1)S(1)}, bf16[256,128]{1,0:T(8,128)(2,1)}, u32[]{:S(2)}) copy-start(bf16[256,128]{1,0:T(8,128)(2,1)} %param.16) | copy-start | bytes 196612
Sparse Core Ops, SparseCore 0:
  10.2 28.7 all-gather.4
  40.8 73.6 all-gather.6

commit v2 on v1

v2 whole, which is shorter than its diff:
```python
import functools
import math

import jax
import jax.numpy as jnp
from jax import lax
from jax.experimental import pallas as pl
from jax.experimental.pallas import tpu as pltpu
from jax.sharding import PartitionSpec as P

CROSS = 2
MESH = pl.DeviceIdType.MESH


def chunk_count(row_count, member_count):
    chunks = 4
    while chunks > 1 and (row_count % (chunks * 128) or member_count % chunks):
        chunks //= 2
    return chunks


def rank_kernel(
    counts, splits,
    feat, weight, bias, tower, tower_bias, query_weight, user, cand, positive,
    out, loss_out,
    x0, x1, flat, sent, rows, towers, biases, columns_bias, queries, cands, losses,
    feat_sem, weight_sem, tower_sem, small_sem,
    right_sem, left_sem, pair_sem, recv_sem, pair_recv,
    row_send, row_recv, chain_right, chain_left, chain_recv, both_send, both_recv,
    plane_send, plane_recv, plane_pair, plane_pair_recv,
    cand_send, cand_recv, loss_send, loss_recv,
):
    batch_count, field_count, dim_count = counts
    chunks, split = splits
    b = lax.axis_index("batch")
    f = lax.axis_index("field")
    d = lax.axis_index("dim")
    me = f * dim_count + d
    members = field_count * dim_count
    fl, el, row_count = feat.shape
    columns = fl * el
    fields, width, rc = x0.shape[1:]
    share = row_count // members
    per_chunk = members // chunks
    part = towers.shape[2]
    units = split * part
    buffers = (x0, x1)
    other = field_count - 1 - f
    mine = b if split > 1 else 0
    to_right = jnp.minimum(d + 1, dim_count - 1)
    to_left = jnp.maximum(d - 1, 0)

    def remote(ref, send, recv, **where):
        return pltpu.make_async_remote_copy(
            ref, ref, send, recv, device_id=where, device_id_type=MESH)

    def place(ff, o):
        return pl.ds(ff * fl, fl), pl.ds(pl.multiple_of(o * el, el), el)

    def piece(ph, c, ff, o):
        fs, ds = place(ff, o)
        return buffers[ph].at[c, fs, ds, :]

    def right(ph, c, o):
        return remote(piece(ph, c, f, o), right_sem.at[ph, c, o], recv_sem.at[ph, c, o], dim=to_right)

    def left(ph, c, o):
        return remote(piece(ph, c, f, o), left_sem.at[ph, c, o], recv_sem.at[ph, c, o], dim=to_left)

    def pair(ph, c, o, ff):
        return remote(
            piece(ph, c, ff, o), pair_sem.at[ph, c, o], pair_recv.at[ph, c, o], field=other)

    def issue_own(ph, c):
        @pl.when(d < dim_count - 1)
        def _():
            right(ph, c, d).start()

        @pl.when(d > 0)
        def _():
            left(ph, c, d).start()

        pair(ph, c, d, f).start()

    def forwards(ph, c):
        for s in range(1, dim_count):
            @pl.when(d - s >= 0)
            def _():
                right(ph, c, d - s).wait_recv()

                @pl.when(d < dim_count - 1)
                def _():
                    right(ph, c, d - s).start()

                pair(ph, c, d - s, f).start()

            @pl.when(d + s < dim_count)
            def _():
                left(ph, c, d + s).wait_recv()

                @pl.when(d > 0)
                def _():
                    left(ph, c, d + s).start()

                pair(ph, c, d + s, f).start()
        for o in range(dim_count):
            pair(ph, c, o, other).wait_recv()

    def weight_copy(level, ff):
        return pltpu.make_async_copy(
            weight.at[level, :, ff],
            flat.at[level, :, :, pl.ds(pl.multiple_of(ff * width, width), width)],
            weight_sem.at[level, ff])

    def tower_copy(ff):
        return pltpu.make_async_copy(
            tower.at[ff, pl.ds(pl.multiple_of(mine * part, part), part), :],
            towers.at[mine, me, :, pl.ds(pl.multiple_of(ff * width, width), width)],
            tower_sem.at[ff])

    def each_field(act):
        def step(ff, carry):
            act(ff)
            return carry

        lax.fori_loop(0, fields, step, 0)

    small_refs = (
        lambda o: towers.at[mine, f * dim_count + o],
        lambda o: queries.at[:, f * dim_count + o],
        lambda o: biases.at[f * dim_count + o],
    )
    small_wide = (
        lambda ff: towers.at[mine, pl.ds(ff * dim_count, dim_count)],
        lambda ff: queries.at[:, pl.ds(ff * dim_count, dim_count)],
        lambda ff: biases.at[pl.ds(ff * dim_count, dim_count)],
    )

    def chain_to(k, o, sems, target):
        return remote(small_refs[k](o), sems.at[k, o], chain_recv.at[k, o], dim=target)

    def chain_own():
        for k in range(3):
            @pl.when(d < dim_count - 1)
            def _():
                chain_to(k, d, chain_right, to_right).start()

            @pl.when(d > 0)
            def _():
                chain_to(k, d, chain_left, to_left).start()

    def chain_step(s):
        for k in range(3):
            @pl.when(d - s >= 0)
            def _():
                chain_to(k, d - s, chain_right, to_right).wait_recv()

                @pl.when(d < dim_count - 1)
                def _():
                    chain_to(k, d - s, chain_right, to_right).start()

            @pl.when(d + s < dim_count)
            def _():
                chain_to(k, d + s, chain_left, to_left).wait_recv()

                @pl.when(d > 0)
                def _():
                    chain_to(k, d + s, chain_left, to_left).start()

    def both(k, ff):
        return remote(small_wide[k](ff), both_send.at[k], both_recv.at[k], field=other)

    def plane(t, source):
        return remote(
            towers.at[source, pl.ds(f * dim_count, dim_count)],
            plane_send.at[t], plane_recv.at[source], batch=t)

    def plane_both(source, ff):
        return remote(
            towers.at[source, pl.ds(ff * dim_count, dim_count)],
            plane_pair.at[source], plane_pair_recv.at[source], field=other)

    def cand_copy(t, source):
        return remote(cands.at[source], cand_send.at[t], cand_recv.at[source], batch=t)

    def loss_copy(m, source):
        return remote(
            losses.at[source], loss_send.at[m], loss_recv.at[source],
            field=m // dim_count, dim=m % dim_count)

    def row_copy(m):
        fs, ds = place(f, d)
        return pltpu.make_async_remote_copy(
            sent.at[m], rows.at[fs, ds, :], row_send.at[m], row_recv.at[me],
            device_id={"field": m // dim_count, "dim": m % dim_count}, device_id_type=MESH)

    def advance(ph, c):
        whole = buffers[ph][c].reshape(fields * width, rc)
        matrix = flat[ph].reshape(columns, fields * width)
        product = jnp.dot(matrix, whole, preferred_element_type=jnp.float32) + bias[ph]
        fs, ds = place(f, d)
        anchor = x0[c, fs, ds, :].astype(jnp.float32).reshape(columns, rc)
        current = buffers[ph][c, fs, ds, :].astype(jnp.float32).reshape(columns, rc)
        return (anchor * product + current).astype(jnp.bfloat16).reshape(fl, el, rc)

    own_copies = []
    for c in range(chunks):
        own_copies.append(pltpu.make_async_copy(
            feat.at[:, :, pl.ds(c * rc, rc)], piece(0, c, f, d), feat_sem.at[c]))
    small_copies = [
        pltpu.make_async_copy(query_weight, queries.at[:, me], small_sem.at[0]),
        pltpu.make_async_copy(tower_bias, biases.at[me], small_sem.at[1]),
        pltpu.make_async_copy(cand, cands.at[b], small_sem.at[2]),
    ]
    for copy in own_copies + small_copies:
        copy.start()
    each_field(lambda ff: tower_copy(ff).start())
    for level in range(CROSS):
        each_field(lambda ff: weight_copy(level, ff).start())

    barrier = pltpu.get_barrier_semaphore()
    for k in range(1, members):
        m = lax.rem(me + k, members)
        pl.semaphore_signal(
            barrier, inc=1, device_id={"field": m // dim_count, "dim": m % dim_count},
            device_id_type=MESH)
    for k in range(1, batch_count):
        pl.semaphore_signal(
            barrier, inc=1, device_id={"batch": lax.rem(b + k, batch_count)}, device_id_type=MESH)
    pl.semaphore_wait(barrier, members + batch_count - 2)
    for copy in own_copies:
        copy.wait()
    issue_own(0, 0)
    if chunks > 1:
        issue_own(0, 1)
    each_field(lambda ff: tower_copy(ff).wait())
    for copy in small_copies:
        copy.wait()
    chain_own()
    for k in range(1, batch_count):
        cand_copy(lax.rem(b + k, batch_count), b).start()
    for level in range(CROSS):
        each_field(lambda ff: weight_copy(level, ff).wait())

    def first(c, carry):
        forwards(0, c)
        fs, ds = place(f, d)
        x1[c, fs, ds, :] = advance(0, c)
        issue_own(1, c)

        @pl.when(c + 2 < chunks)
        def _():
            issue_own(0, c + 2)

        for s in range(1, min(chunks, dim_count)):
            @pl.when(c == s)
            def _():
                chain_step(s)

        return carry

    lax.fori_loop(0, chunks, first, 0)
    for s in range(min(chunks, dim_count), dim_count):
        chain_step(s)
    for k in range(3):
        both(k, f).start()
    if split > 1:
        for k in range(1, split):
            plane(lax.rem(b + k, split), b).start()

    def second(c, carry):
        forwards(1, c)
        new = advance(1, c)
        out[:, :, pl.ds(pl.multiple_of(c * rc, 128), rc)] = new
        for j in range(per_chunk):
            m = c * per_chunk + j
            piece_rows = new[:, :, j * share:(j + 1) * share]

            @pl.when(m == me)
            def _():
                fs, ds = place(f, d)
                rows[fs, ds, :] = piece_rows

            @pl.when(m != me)
            def _():
                sent[m] = piece_rows
                row_copy(m).start()

        return carry

    lax.fori_loop(0, chunks, second, 0)

    if split > 1:
        for k in range(1, split):
            source = lax.rem(b + k, split)
            plane(source, source).wait_recv()
            plane_both(source, f).start()
    for k in range(3):
        both(k, other).wait_recv()
    for k in range(1, batch_count):
        source = lax.rem(b + k, batch_count)
        cand_copy(source, source).wait_recv()
    for m in range(members):
        block = jnp.broadcast_to(biases[m], (share, units)).T
        columns_bias[:, m] = block.reshape(split, part, share)
    if split > 1:
        for k in range(1, split):
            plane_both(lax.rem(b + k, split), other).wait_recv()
    for k in range(1, members):
        m = lax.rem(me + k, members)
        fs, ds = place(m // dim_count, m % dim_count)
        remote(rows.at[fs, ds, :], row_send.at[m], row_recv.at[m],
               field=m // dim_count, dim=m % dim_count).wait_recv()

    def tower_block(s, query):
        matrix = towers[s].reshape(members * part, fields * width)
        pre = jnp.dot(
            matrix, rows[...].reshape(fields * width, share), preferred_element_type=jnp.float32)
        pre = pre + columns_bias[s].reshape(members * part, share)
        hidden = jnp.maximum(pre, 0.0).astype(jnp.bfloat16)
        return query + lax.dot_general(
            hidden, queries[s].reshape(members * part, width), (((0,), (0,)), ((), ())),
            preferred_element_type=jnp.float32)

    query = lax.fori_loop(0, split, tower_block, jnp.zeros((share, width), jnp.float32))
    start = pl.multiple_of(me * share, share)
    query_vec = (query + user[pl.ds(start, share), :].astype(jnp.float32)).astype(jnp.bfloat16)
    all_cands = cands[...].reshape(-1, width)
    logits = lax.dot_general(
        all_cands, query_vec, (((1,), (1,)), ((), ())), preferred_element_type=jnp.float32
    ) * (1.0 / math.sqrt(width))
    labels = lax.broadcasted_iota(jnp.int32, logits.shape, 0)
    picked = jnp.sum(jnp.where(labels == positive[me], logits, 0.0), axis=0, keepdims=True)
    best = jnp.max(logits, axis=0, keepdims=True)
    total = jnp.sum(jnp.exp(logits - best), axis=0, keepdims=True)
    losses[me] = best + jnp.log(total) - picked
    for k in range(1, members):
        loss_copy(lax.rem(me + k, members), me).start()

    def drain(c, carry):
        for ph in range(CROSS):
            for o in range(dim_count):
                @pl.when((o <= d) & (d < dim_count - 1))
                def _():
                    right(ph, c, o).wait_send()

                @pl.when((o >= d) & (d > 0))
                def _():
                    left(ph, c, o).wait_send()

                pair(ph, c, o, f).wait_send()
        return carry

    lax.fori_loop(0, chunks, drain, 0)
    for k in range(3):
        for o in range(dim_count):
            @pl.when((o <= d) & (d < dim_count - 1))
            def _():
                chain_to(k, o, chain_right, to_right).wait_send()

            @pl.when((o >= d) & (d > 0))
            def _():
                chain_to(k, o, chain_left, to_left).wait_send()

        both(k, f).wait_send()
    if split > 1:
        for k in range(1, split):
            t = lax.rem(b + k, split)
            plane(t, b).wait_send()
            plane_both(t, f).wait_send()
    for k in range(1, batch_count):
        cand_copy(lax.rem(b + k, batch_count), b).wait_send()
    for k in range(1, members):
        m = lax.rem(me + k, members)
        row_copy(m).wait_send()
        loss_copy(m, m).wait_recv()
        loss_copy(m, me).wait_send()
    loss_out[...] = losses[...]


def body(
    features, cross_weight, cross_bias, tower_weight, tower_bias, query_weight,
    user_vec, candidates, positive,
):
    counts = tuple(lax.axis_size(name) for name in ("batch", "field", "dim"))
    batch_count, field_count, dim_count = counts
    members = field_count * dim_count
    fl, el, row_count = features.shape
    columns = fl * el
    units, fields, width = tower_weight.shape
    chunks = chunk_count(row_count, members)
    split = batch_count if units % (batch_count * 16) == 0 else 1
    part = units // split
    rc = row_count // chunks
    share = row_count // members
    steps = (CROSS, chunks, dim_count)
    small = (3, dim_count)
    dma = pltpu.SemaphoreType.DMA
    vmem = pltpu.VMEM
    bf16 = jnp.bfloat16
    far = pl.BlockSpec(memory_space=pl.ANY)
    near = pl.BlockSpec(memory_space=pltpu.VMEM)
    crossed, losses = pl.pallas_call(
        functools.partial(rank_kernel, counts, (chunks, split)),
        out_shape=(
            jax.ShapeDtypeStruct(features.shape, bf16),
            jax.ShapeDtypeStruct((members, 1, share), jnp.float32),
        ),
        in_specs=[far, far, near, far, far, far, near, far, near],
        out_specs=(near, near),
        scratch_shapes=[
            vmem((chunks, fields, width, rc), bf16),
            vmem((chunks, fields, width, rc), bf16),
            vmem((CROSS, fl, el, fields * width), bf16),
            vmem((members, fl, el, share), bf16),
            vmem((fields, width, share), bf16),
            vmem((split, members, part, fields * width), bf16),
            vmem((members, 1, units), jnp.float32),
            vmem((split, members, part, share), jnp.float32),
            vmem((split, members, part, width), bf16),
            vmem((batch_count,) + candidates.shape, bf16),
            vmem((members, 1, share), jnp.float32),
            dma((chunks,)), dma((CROSS, fields)), dma((fields,)), dma((3,)),
            dma(steps), dma(steps), dma(steps), dma(steps), dma(steps),
            dma((members,)), dma((members,)), dma(small), dma(small), dma(small),
            dma((3,)), dma((3,)),
            dma((split,)), dma((split,)), dma((split,)), dma((split,)),
            dma((batch_count,)), dma((batch_count,)), dma((members,)), dma((members,)),
        ],
        compiler_params=pltpu.CompilerParams(
            collective_id=0, has_side_effects=True, vmem_limit_bytes=56 * 2**20),
        name="rank_forward",
    )(
        features,
        cross_weight.transpose(0, 1, 3, 2, 4),
        cross_bias.reshape(CROSS, columns, 1),
        tower_weight.transpose(1, 0, 2),
        tower_bias.reshape(1, units),
        query_weight.reshape(split, part, width),
        user_vec,
        candidates,
        positive.reshape(members, 1, share),
    )
    return (crossed, losses.reshape(row_count))


def solution(mesh):
    placed = (
        P("field", "dim", "batch"),
        P(None, "field", "dim", None, None),
        P(None, "field", "dim"),
        P(("field", "dim"), None, None),
        P(("field", "dim")),
        P(("field", "dim"), None),
        P("batch", None),
        P("batch", None),
        P("batch"),
    )
    return jax.shard_map(
        body,
        mesh=mesh,
        in_specs=placed,
        out_specs=(P("field", "dim", "batch"), P("batch")),
        check_vma=False,
    )
```

time: 278 us -> 175 us (0.63)
  blocking collectives: 63.7 us -> 0 us
  waiting for transfers between devices: 28.9 us -> 0 us
  Pallas kernels: 150 us -> 169 us
  between operations: 14.1 us -> 0.64 us
  local copies, waits for them, and re-layouts: 14.4 us -> 5.3 us
  matrix products: 6.33 us -> 0 us
    all_gather x4 -> x0, blocking collectives: 63.7 us -> none  [the longest x1 25.1 us: body(): lax.all_gather(query_weight, ('field', 'dim'), axis=0, tiled=True)]
    all_gather x2 -> x0, waiting for transfers between devices: 28.8 us -> none  [the longest x1 28.8 us: spread(): level = lax.all_gather(mine, ('field', 'dim'), axis=0, tiled=True)]
    pallas_call x1, Pallas kernels: 150 us -> 169 us  [body(): pl.pallas_call(functools.partial(rank_kernel, counts, (chunks, split)), o...]
    unnamed x13 -> x3, local copies, waits for them, and re-layouts: 11.3 us -> 4.1 us
    dot_general x2 -> x0, matrix products: 6.33 us -> none  [the longest x1 5.04 us: body(): jnp.dot(tower_all, rows.reshape(fields * width, share), preferred_element...]
  transfers between devices with their start and end apart: 2 -> 0, of which waited for: 1 -> 0; matrix products, arithmetic and copies ran while one was open for 4% -> 0% of each run, Pallas kernels for 54% -> 0%
where the time goes in v2:
time: 175 us
  Pallas kernels  169 us (97%)
  local copies, waits for them, and re-layouts  5.3 us (3%)
    pallas_call x1, Pallas kernels, body(): pl.pallas_call(functools.partial(rank_kernel, counts, (chunks, split)), o...  169 us
    unnamed x3, local copies, waits for them, and re-layouts  4.1 us

profile of v2, /device:TPU:0, one launch (start us, length us, event | category | flops | bytes accessed | tf_op | source)
XLA Modules:
  0.0 174.8 jit_solution(9668900893191691738)
XLA Ops:
  0.6 0.7 copy.12
  1.3 1.2 reshape.24.bias
  2.5 168.9 %rank_forward.1 = (bf16[13,32,1024]{2,1,0:T(8,128)(2,1)}, f32[8,1,128]{2,1,0:T(1,128)}) custom-call(bf16[13,32,1024]{2,1,0:T(8,128)(2,1)} %feat.1, bf16[2,13,26,32,128]{4,3,2,1,0:T(8,128)(2,1)} %bitcast.6, f32[2,416,1]{2,1,0:T(8,128)} %reshape.24.bias, bf16[26,128,128]{2,1,0:T(8,128)(2,1)} %bitcast.7, f32[1,128]{1,0:T(1,128)} %bitcast.11, ...), custom_call_target="tpu_custom_call" | custom-call | tf_op jit(solution)/shard_map/rank_forward/pallas_call | solution.py:403
  171.4 2.1 %copy.16 = bf16[13,32,1024]{2,1,0:T(8,128)(2,1)} copy(bf16[13,32,1024]{2,1,0:T(8,128)(2,1)} %get-tuple-element.8) | data formatting | bytes 1703936
  173.5 1.3 copy.17

commit v3 on v2

--- a/solution.py
+++ b/solution.py
@@ -12,9 +12,14 @@
 MESH = pl.DeviceIdType.MESH
 
 
-def chunk_count(row_count, member_count):
+def tower_levels(dim_count):
+    held = min(2, dim_count)
+    return (dim_count - held) // 2, held
+
+
+def chunk_count(row_count, field_count, held):
     chunks = 4
-    while chunks > 1 and (row_count % (chunks * 128) or member_count % chunks):
+    while chunks > field_count and row_count % (chunks * held * 128):
         chunks //= 2
     return chunks
 
@@ -40,8 +45,13 @@
     fl, el, row_count = feat.shape
     columns = fl * el
     fields, width, rc = x0.shape[1:]
-    share = row_count // members
-    per_chunk = members // chunks
+    low, held = tower_levels(dim_count)
+    high = low + held - 1
+    level_of = d - low
+    active = (d >= low) & (d <= high)
+    sub = rc // held
+    run = chunks // field_count
+    share = run * sub
     part = towers.shape[2]
     units = split * part
     buffers = (x0, x1)
@@ -141,29 +151,29 @@
 
     def chain_own():
         for k in range(3):
-            @pl.when(d < dim_count - 1)
+            @pl.when(d < high)
             def _():
                 chain_to(k, d, chain_right, to_right).start()
 
-            @pl.when(d > 0)
+            @pl.when(d > low)
             def _():
                 chain_to(k, d, chain_left, to_left).start()
 
     def chain_step(s):
         for k in range(3):
-            @pl.when(d - s >= 0)
+            @pl.when((d - s >= 0) & (d <= high))
             def _():
                 chain_to(k, d - s, chain_right, to_right).wait_recv()
 
-                @pl.when(d < dim_count - 1)
+                @pl.when(d < high)
                 def _():
                     chain_to(k, d - s, chain_right, to_right).start()
 
-            @pl.when(d + s < dim_count)
+            @pl.when((d + s < dim_count) & (d >= low))
             def _():
                 chain_to(k, d + s, chain_left, to_left).wait_recv()
 
-                @pl.when(d > 0)
+                @pl.when(d > low)
                 def _():
                     chain_to(k, d + s, chain_left, to_left).start()
 
@@ -183,16 +193,21 @@
     def cand_copy(t, source):
         return remote(cands.at[source], cand_send.at[t], cand_recv.at[source], batch=t)
 
-    def loss_copy(m, source):
+    def loss_copy(m, ff, level):
+        ref = losses.at[level, pl.ds(ff * run, run)]
         return remote(
-            losses.at[source], loss_send.at[m], loss_recv.at[source],
-            field=m // dim_count, dim=m % dim_count)
-
-    def row_copy(m):
+            ref, loss_send.at[m], loss_recv.at[ff, level], field=m // dim_count, dim=m % dim_count)
+
+    def row_copy(c, level):
         fs, ds = place(f, d)
         return pltpu.make_async_remote_copy(
-            sent.at[m], rows.at[fs, ds, :], row_send.at[m], row_recv.at[me],
-            device_id={"field": m // dim_count, "dim": m % dim_count}, device_id_type=MESH)
+            sent.at[c, level],
+            rows.at[fs, ds, pl.ds(pl.multiple_of(lax.rem(c, run) * sub, sub), sub)],
+            row_send.at[c, level], row_recv.at[lax.rem(c, run), me],
+            device_id={"field": c // run, "dim": low + level}, device_id_type=MESH)
+
+    def own_rows(c, level):
+        return (c // run == f) & (level_of == level)
 
     def advance(ph, c):
         whole = buffers[ph][c].reshape(fields * width, rc)
@@ -237,8 +252,12 @@
     for copy in small_copies:
         copy.wait()
     chain_own()
-    for k in range(1, batch_count):
-        cand_copy(lax.rem(b + k, batch_count), b).start()
+
+    @pl.when(active)
+    def _():
+        for k in range(1, batch_count):
+            cand_copy(lax.rem(b + k, batch_count), b).start()
+
     for level in range(CROSS):
         each_field(lambda ff: weight_copy(level, ff).wait())
 
@@ -262,55 +281,35 @@
     lax.fori_loop(0, chunks, first, 0)
     for s in range(min(chunks, dim_count), dim_count):
         chain_step(s)
-    for k in range(3):
-        both(k, f).start()
-    if split > 1:
-        for k in range(1, split):
-            plane(lax.rem(b + k, split), b).start()
+
+    @pl.when(active)
+    def _():
+        for k in range(3):
+            both(k, f).start()
+        if split > 1:
+            for k in range(1, split):
+                plane(lax.rem(b + k, split), b).start()
 
     def second(c, carry):
         forwards(1, c)
         new = advance(1, c)
         out[:, :, pl.ds(pl.multiple_of(c * rc, 128), rc)] = new
-        for j in range(per_chunk):
-            m = c * per_chunk + j
-            piece_rows = new[:, :, j * share:(j + 1) * share]
-
-            @pl.when(m == me)
+        for level in range(held):
+            block = new[:, :, level * sub:(level + 1) * sub]
+
+            @pl.when(own_rows(c, level))
             def _():
                 fs, ds = place(f, d)
-                rows[fs, ds, :] = piece_rows
-
-            @pl.when(m != me)
-            def _():
-                sent[m] = piece_rows
-                row_copy(m).start()
+                rows[fs, ds, pl.ds(pl.multiple_of(lax.rem(c, run) * sub, sub), sub)] = block
+
+            @pl.when(jnp.logical_not(own_rows(c, level)))
+            def _():
+                sent[c, level] = block
+                row_copy(c, level).start()
 
         return carry
 
     lax.fori_loop(0, chunks, second, 0)
-
-    if split > 1:
-        for k in range(1, split):
-            source = lax.rem(b + k, split)
-            plane(source, source).wait_recv()
-            plane_both(source, f).start()
-    for k in range(3):
-        both(k, other).wait_recv()
-    for k in range(1, batch_count):
-        source = lax.rem(b + k, batch_count)
-        cand_copy(source, source).wait_recv()
-    for m in range(members):
-        block = jnp.broadcast_to(biases[m], (share, units)).T
-        columns_bias[:, m] = block.reshape(split, part, share)
-    if split > 1:
-        for k in range(1, split):
-            plane_both(lax.rem(b + k, split), other).wait_recv()
-    for k in range(1, members):
-        m = lax.rem(me + k, members)
-        fs, ds = place(m // dim_count, m % dim_count)
-        remote(rows.at[fs, ds, :], row_send.at[m], row_recv.at[m],
-               field=m // dim_count, dim=m % dim_count).wait_recv()
 
     def tower_block(s, query):
         matrix = towers[s].reshape(members * part, fields * width)
@@ -322,20 +321,50 @@
             hidden, queries[s].reshape(members * part, width), (((0,), (0,)), ((), ())),
             preferred_element_type=jnp.float32)
 
-    query = lax.fori_loop(0, split, tower_block, jnp.zeros((share, width), jnp.float32))
-    start = pl.multiple_of(me * share, share)
-    query_vec = (query + user[pl.ds(start, share), :].astype(jnp.float32)).astype(jnp.bfloat16)
-    all_cands = cands[...].reshape(-1, width)
-    logits = lax.dot_general(
-        all_cands, query_vec, (((1,), (1,)), ((), ())), preferred_element_type=jnp.float32
-    ) * (1.0 / math.sqrt(width))
-    labels = lax.broadcasted_iota(jnp.int32, logits.shape, 0)
-    picked = jnp.sum(jnp.where(labels == positive[me], logits, 0.0), axis=0, keepdims=True)
-    best = jnp.max(logits, axis=0, keepdims=True)
-    total = jnp.sum(jnp.exp(logits - best), axis=0, keepdims=True)
-    losses[me] = best + jnp.log(total) - picked
-    for k in range(1, members):
-        loss_copy(lax.rem(me + k, members), me).start()
+    @pl.when(active)
+    def _():
+        if split > 1:
+            for k in range(1, split):
+                source = lax.rem(b + k, split)
+                plane(source, source).wait_recv()
+                plane_both(source, f).start()
+        for k in range(3):
+            both(k, other).wait_recv()
+        for k in range(1, batch_count):
+            source = lax.rem(b + k, batch_count)
+            cand_copy(source, source).wait_recv()
+        for m in range(members):
+            block = jnp.broadcast_to(biases[m], (share, units)).T
+            columns_bias[:, m] = block.reshape(split, part, share)
+        if split > 1:
+            for k in range(1, split):
+                plane_both(lax.rem(b + k, split), other).wait_recv()
+        for j in range(run):
+            for k in range(1, members):
+                m = lax.rem(me + k, members)
+                fs, ds = place(m // dim_count, m % dim_count)
+                remote(rows.at[fs, ds, pl.ds(j * sub, sub)], row_send.at[0, 0], row_recv.at[j, m],
+                       field=m // dim_count, dim=m % dim_count).wait_recv()
+
+        query = lax.fori_loop(0, split, tower_block, jnp.zeros((share, width), jnp.float32))
+        all_cands = cands[...].reshape(-1, width)
+        for j in range(run):
+            c = f * run + j
+            start = pl.multiple_of(c * rc + level_of * sub, sub)
+            query_vec = (
+                query[j * sub:(j + 1) * sub] + user[pl.ds(start, sub), :].astype(jnp.float32)
+            ).astype(jnp.bfloat16)
+            logits = lax.dot_general(
+                all_cands, query_vec, (((1,), (1,)), ((), ())), preferred_element_type=jnp.float32
+            ) * (1.0 / math.sqrt(width))
+            labels = lax.broadcasted_iota(jnp.int32, logits.shape, 0)
+            target = positive[c * held + level_of]
+            picked = jnp.sum(jnp.where(labels == target, logits, 0.0), axis=0, keepdims=True)
+            best = jnp.max(logits, axis=0, keepdims=True)
+            total = jnp.sum(jnp.exp(logits - best), axis=0, keepdims=True)
+            losses[level_of, c] = best + jnp.log(total) - picked
+        for k in range(1, members):
+            loss_copy(lax.rem(me + k, members), f, level_of).start()
 
     def drain(c, carry):
         for ph in range(CROSS):
@@ -354,28 +383,43 @@
     lax.fori_loop(0, chunks, drain, 0)
     for k in range(3):
         for o in range(dim_count):
-            @pl.when((o <= d) & (d < dim_count - 1))
+            @pl.when((o <= d) & (d < high))
             def _():
                 chain_to(k, o, chain_right, to_right).wait_send()
 
-            @pl.when((o >= d) & (d > 0))
+            @pl.when((o >= d) & (d > low))
             def _():
                 chain_to(k, o, chain_left, to_left).wait_send()
 
-        both(k, f).wait_send()
-    if split > 1:
-        for k in range(1, split):
-            t = lax.rem(b + k, split)
-            plane(t, b).wait_send()
-            plane_both(t, f).wait_send()
-    for k in range(1, batch_count):
-        cand_copy(lax.rem(b + k, batch_count), b).wait_send()
-    for k in range(1, members):
-        m = lax.rem(me + k, members)
-        row_copy(m).wait_send()
-        loss_copy(m, m).wait_recv()
-        loss_copy(m, me).wait_send()
-    loss_out[...] = losses[...]
+    @pl.when(active)
+    def _():
+        for k in range(3):
+            both(k, f).wait_send()
+        if split > 1:
+            for k in range(1, split):
+                t = lax.rem(b + k, split)
+                plane(t, b).wait_send()
+                plane_both(t, f).wait_send()
+        for k in range(1, batch_count):
+            cand_copy(lax.rem(b + k, batch_count), b).wait_send()
+        for k in range(1, members):
+            loss_copy(lax.rem(me + k, members), f, level_of).wait_send()
+
+    for c in range(chunks):
+        for level in range(held):
+            @pl.when(jnp.logical_not(own_rows(c, level)))
+            def _():
+                row_copy(c, level).wait_send()
+
+    for ff in range(field_count):
+        for level in range(held):
+            @pl.when(jnp.logical_not((f == ff) & (level_of == level)))
+            def _():
+                loss_copy(ff * dim_count + low + level, ff, level).wait_recv()
+
+    for c in range(chunks):
+        for level in range(held):
+            loss_out[c * held + level] = losses[level, c]
 
 
 def body(
@@ -388,11 +432,14 @@
     fl, el, row_count = features.shape
     columns = fl * el
     units, fields, width = tower_weight.shape
-    chunks = chunk_count(row_count, members)
+    low, held = tower_levels(dim_count)
+    chunks = chunk_count(row_count, field_count, held)
     split = batch_count if units % (batch_count * 16) == 0 else 1
     part = units // split
     rc = row_count // chunks
-    share = row_count // members
+    sub = rc // held
+    run = chunks // field_count
+    share = run * sub
     steps = (CROSS, chunks, dim_count)
     small = (3, dim_count)
     dma = pltpu.SemaphoreType.DMA
@@ -404,7 +451,7 @@
         functools.partial(rank_kernel, counts, (chunks, split)),
         out_shape=(
             jax.ShapeDtypeStruct(features.shape, bf16),
-            jax.ShapeDtypeStruct((members, 1, share), jnp.float32),
+            jax.ShapeDtypeStruct((chunks * held, 1, sub), jnp.float32),
         ),
         in_specs=[far, far, near, far, far, far, near, far, near],
         out_specs=(near, near),
@@ -412,20 +459,20 @@
             vmem((chunks, fields, width, rc), bf16),
             vmem((chunks, fields, width, rc), bf16),
             vmem((CROSS, fl, el, fields * width), bf16),
-            vmem((members, fl, el, share), bf16),
+            vmem((chunks, held, fl, el, sub), bf16),
             vmem((fields, width, share), bf16),
             vmem((split, members, part, fields * width), bf16),
             vmem((members, 1, units), jnp.float32),
             vmem((split, members, part, share), jnp.float32),
             vmem((split, members, part, width), bf16),
             vmem((batch_count,) + candidates.shape, bf16),
-            vmem((members, 1, share), jnp.float32),
+            vmem((held, chunks, 1, sub), jnp.float32),
             dma((chunks,)), dma((CROSS, fields)), dma((fields,)), dma((3,)),
             dma(steps), dma(steps), dma(steps), dma(steps), dma(steps),
-            dma((members,)), dma((members,)), dma(small), dma(small), dma(small),
+            dma((chunks, held)), dma((run, members)), dma(small), dma(small), dma(small),
             dma((3,)), dma((3,)),
             dma((split,)), dma((split,)), dma((split,)), dma((split,)),
-            dma((batch_count,)), dma((batch_count,)), dma((members,)), dma((members,)),
+            dma((batch_count,)), dma((batch_count,)), dma((members,)), dma((field_count, held)),
         ],
         compiler_params=pltpu.CompilerParams(
             collective_id=0, has_side_effects=True, vmem_limit_bytes=56 * 2**20),
@@ -439,7 +486,7 @@
         query_weight.reshape(split, part, width),
         user_vec,
         candidates,
-        positive.reshape(members, 1, share),
+        positive.reshape(chunks * held, 1, sub),
     )
     return (crossed, losses.reshape(row_count))
 

time: 175 us -> 160 us (0.914)
  Pallas kernels: 169 us -> 154 us
    pallas_call x1, Pallas kernels: 169 us -> 154 us  [body(): pl.pallas_call(functools.partial(rank_kernel, counts, (chunks, split)), o...]
where the time goes in v3:
time: 160 us
  Pallas kernels  154 us (96%)
  local copies, waits for them, and re-layouts  5.3 us (3%)
    pallas_call x1, Pallas kernels, body(): pl.pallas_call(functools.partial(rank_kernel, counts, (chunks, split)), o...  154 us
    unnamed x3, local copies, waits for them, and re-layouts  4.1 us

profile of v3, /device:TPU:0, one launch (start us, length us, event | category | flops | bytes accessed | tf_op | source)
XLA Modules:
  0.0 159.7 jit_solution(16039986046546694868)
XLA Ops:
  0.6 0.7 copy.12
  1.3 1.2 reshape.24.bias
  2.5 153.7 %rank_forward.1 = (bf16[13,32,1024]{2,1,0:T(8,128)(2,1)}, f32[8,1,128]{2,1,0:T(1,128)}) custom-call(bf16[13,32,1024]{2,1,0:T(8,128)(2,1)} %feat.1, bf16[2,13,26,32,128]{4,3,2,1,0:T(8,128)(2,1)} %bitcast.6, f32[2,416,1]{2,1,0:T(8,128)} %reshape.24.bias, bf16[26,128,128]{2,1,0:T(8,128)(2,1)} %bitcast.7, f32[1,128]{1,0:T(1,128)} %bitcast.11, ...), custom_call_target="tpu_custom_call" | custom-call | tf_op jit(solution)/shard_map/rank_forward/pallas_call | solution.py:450
  156.3 2.1 %copy.16 = bf16[13,32,1024]{2,1,0:T(8,128)(2,1)} copy(bf16[13,32,1024]{2,1,0:T(8,128)(2,1)} %get-tuple-element.8) | data formatting | bytes 1703936
  158.4 1.3 copy.17

commit v4 on v3

--- a/solution.py
+++ b/solution.py
@@ -18,7 +18,7 @@
 
 
 def chunk_count(row_count, field_count, held):
-    chunks = 4
+    chunks = 2
     while chunks > field_count and row_count % (chunks * held * 128):
         chunks //= 2
     return chunks
@@ -262,14 +262,14 @@
         each_field(lambda ff: weight_copy(level, ff).wait())
 
     def first(c, carry):
+        @pl.when(c + 2 < chunks)
+        def _():
+            issue_own(0, c + 2)
+
         forwards(0, c)
         fs, ds = place(f, d)
         x1[c, fs, ds, :] = advance(0, c)
         issue_own(1, c)
-
-        @pl.when(c + 2 < chunks)
-        def _():
-            issue_own(0, c + 2)
 
         for s in range(1, min(chunks, dim_count)):
             @pl.when(c == s)

time: 160 us -> 154 us (0.963)
  Pallas kernels: 154 us -> 148 us
    pallas_call x1, Pallas kernels: 154 us -> 148 us  [body(): pl.pallas_call(functools.partial(rank_kernel, counts, (chunks, split)), o...]
where the time goes in v4:
time: 154 us
  Pallas kernels  148 us (96%)
  local copies, waits for them, and re-layouts  5.3 us (3%)
    pallas_call x1, Pallas kernels, body(): pl.pallas_call(functools.partial(rank_kernel, counts, (chunks, split)), o...  148 us
    unnamed x3, local copies, waits for them, and re-layouts  4.1 us

profile of v4, /device:TPU:0, one launch (start us, length us, event | category | flops | bytes accessed | tf_op | source)
XLA Modules:
  0.0 153.5 jit_solution(7235508768854950380)
XLA Ops:
  0.6 0.7 copy.12
  1.3 1.2 reshape.24.bias
  2.5 147.6 %rank_forward.1 = (bf16[13,32,1024]{2,1,0:T(8,128)(2,1)}, f32[4,1,256]{2,1,0:T(1,128)}) custom-call(bf16[13,32,1024]{2,1,0:T(8,128)(2,1)} %feat.1, bf16[2,13,26,32,128]{4,3,2,1,0:T(8,128)(2,1)} %bitcast.6, f32[2,416,1]{2,1,0:T(8,128)} %reshape.24.bias, bf16[26,128,128]{2,1,0:T(8,128)(2,1)} %bitcast.7, f32[1,128]{1,0:T(1,128)} %bitcast.11, ...), custom_call_target="tpu_custom_call" | custom-call | tf_op jit(solution)/shard_map/rank_forward/pallas_call | solution.py:450
  150.1 2.1 %copy.16 = bf16[13,32,1024]{2,1,0:T(8,128)(2,1)} copy(bf16[13,32,1024]{2,1,0:T(8,128)(2,1)} %get-tuple-element.8) | data formatting | bytes 1703936
  152.3 1.3 copy.17
